TPU v7x, 32 devices: a whole 2x2x4 slice. The times are simulated.
32 devices in a mesh: wrow: 4 (over y, core), wcol: 2 (over x), dom: 4 (over z).
Axes of the slice: x: 2, y: 2, z: 4, core: 2. Of those that a mesh axis runs over, the one named last changes fastest.
Arguments:
- positions: float32 [4, 2, 3, 8192], P('wrow', 'wcol', None, 'dom'), may hold values from -6 to 6
- velocities: float32 [4, 2, 3, 8192], P('wrow', 'wcol', None, 'dom'), may hold values from -6 to 6
- inv_mass: float32 [8192], P('dom'), may hold values from 0.5 to 2
- cv_weight: float32 [2, 3, 8192], P(None, None, 'dom'), may hold values from -0.125 to 0.125
- stiffness: float32 [2], replicated, may hold values from 1 to 4
- centers: float32 [4, 2, 2], P('wrow', 'wcol'), may hold values from -3 to 3
- block_order: int32 [8192], P('dom'), may hold values from 0 to 2047, as said below
- pair_count: int32 [4], P('dom'), may hold values from 16 to 64, as said below
- pair_own: int32 [4, 64], P('dom'), may hold values from 0 to 15, as said below
- pair_other: int32 [4, 64], P('dom'), may hold values from 0 to 47, as said below
- accept_row: int32 [4, 2], P('wrow', 'wcol'), may hold values from 0 to 1, as said below
- accept_col: int32 [4, 2], P('wrow', 'wcol'), may hold values from 0 to 1, as said below
Outputs:
- new_positions: float32 [4, 2, 3, 8192], P('wrow', 'wcol', None, 'dom')
- new_velocities: float32 [4, 2, 3, 8192], P('wrow', 'wcol', None, 'dom')
- new_forces: float32 [4, 2, 3, 8192], P('wrow', 'wcol', None, 'dom')
Inputs may be any that keep to these rules, and one draw needn't show every extreme that they name: accept_row is equal for windows (2k, c) and (2k + 1, c). accept_col is equal for windows (r, 2k) and (r, 2k + 1). `block_order`: each slab's 2048 entries are a permutation of 0 to 2047. `pair_count`: some slab has exactly 64 live pairs. `pair_own`: entries past the slab's pair_count are 0. `pair_other`: slab 0 names no lower slab and the last slab no upper slab; entries past the slab's pair_count are 16.
All inputs are finite; a program needn't handle non-finite values.
Results may differ from a plain program's by a relative error of at most 0.0003.
Values sent between devices are 32-bit elements; how exact they have to be, the bound alone decides.
A program may use at most 64 MiB of HBM per device.

v0:
```python
import math

import jax
import jax.numpy as jnp
from jax import lax
from jax.sharding import PartitionSpec as P

BLK = 128
STEPS = 3


PAIR_EPS = 0.015625
DT = 0.1


def extended(cells, sides, width):
    for axis, dim in sides:
        count = lax.axis_size(axis)
        ends = count - 1
        head = lax.slice_in_dim(cells, 0, width, axis=dim)
        tail = lax.slice_in_dim(cells, cells.shape[dim] - width, cells.shape[dim], axis=dim)
        cells = jnp.concatenate(
            [
                lax.ppermute(tail, axis, [(i, (i + 1) % count) for i in range(ends)]),
                cells,
                lax.ppermute(head, axis, [((i + 1) % count, i) for i in range(ends)]),
            ],
            axis=dim,
        )
    return cells


def from_partner(value, axis, apart):
    mask = 2**apart
    pairs = [(source, source ^ mask) for source in range(lax.axis_size(axis))]
    return lax.ppermute(value, axis, pairs)


def pair_batch(own_tiles, other_tiles):
    offsets = own_tiles[:, :, :, None] - other_tiles[:, :, None, :]
    squared = jnp.sum(offsets * offsets, axis=1)
    weight_tiles = PAIR_EPS * jnp.exp(-0.5 * squared)
    pulled = jnp.einsum("gcj,gij->gci", other_tiles, weight_tiles, precision=lax.Precision.HIGHEST)
    return own_tiles * jnp.sum(weight_tiles, axis=2)[:, None, :] - pulled


def per_device(
    positions,
    velocities,
    inv_mass,
    cv_weight,
    stiffness,
    centers,
    block_order,
    pair_count,
    pair_own,
    pair_other,
    accept_row,
    accept_col,
):
    atom_dev = block_order.shape[0]
    blocks_dev = atom_dev // BLK
    slots = pair_own.shape[1]
    group_size = math.gcd(slots, 32)
    groups = slots // group_size
    coords = positions[0, 0][:, block_order]
    speeds = velocities[0, 0][:, block_order]
    inverse_mass = inv_mass[block_order]
    weights = cv_weight[:, :, block_order]
    centre_pair = centers[0, 0]
    pair_total = pair_count[0]
    own_blocks = pair_own[0]
    other_blocks = pair_other[0]
    live_slots = jnp.arange(slots, dtype=jnp.int32) < pair_total
    owner_table = (
        (jnp.arange(blocks_dev, dtype=jnp.int32)[:, None] == own_blocks[None, :])
        & live_slots[None, :]
    ).astype(jnp.float32)

    def local_cv(current):
        return jnp.sum(weights * current[None], axis=(1, 2))

    def force_from(collective, nearby, centre_now):
        block_view = jnp.transpose(nearby.reshape(3, 3 * blocks_dev, BLK), (1, 0, 2))
        own_tiles = block_view[own_blocks + blocks_dev].reshape(groups, group_size, 3, BLK)
        other_tiles = block_view[other_blocks].reshape(groups, group_size, 3, BLK)
        tiles = lax.map(lambda pieces: pair_batch(pieces[0], pieces[1]), (own_tiles, other_tiles))
        tiles = tiles.reshape(slots, 3 * BLK)
        summed = jnp.dot(owner_table, tiles, precision=lax.Precision.HIGHEST)
        pair = jnp.transpose(summed.reshape(blocks_dev, 3, BLK), (1, 0, 2)).reshape(3, atom_dev)
        pull = stiffness * (collective - centre_now)
        return pair - jnp.sum(pull[:, None, None] * weights, axis=0)

    def total_force(current):
        collective = lax.psum(local_cv(current), "dom")
        nearby = extended(current, (("dom", 1),), atom_dev)
        return force_from(collective, nearby, centre_pair)

    forces_now = total_force(coords)
    for _ in range(STEPS):
        speeds = speeds + 0.5 * DT * inverse_mass * forces_now
        coords = coords + DT * speeds
        forces_now = total_force(coords)
        speeds = speeds + 0.5 * DT * inverse_mass * forces_now
    inverse = (
        jnp.zeros((atom_dev,), jnp.int32).at[block_order].set(jnp.arange(atom_dev, dtype=jnp.int32))
    )
    stacked = jnp.stack([coords, speeds, forces_now])
    partner = from_partner(stacked, "wrow", 0)
    stacked = jnp.where(accept_row[0, 0] == 1, partner, stacked)
    partner = from_partner(stacked, "wcol", 0)
    stacked = jnp.where(accept_col[0, 0] == 1, partner, stacked)
    stacked = stacked[:, :, inverse]
    return (stacked[0][None, None], stacked[1][None, None], stacked[2][None, None])


def solution(mesh):
    placed = (
        P("wrow", "wcol", None, "dom"),
        P("wrow", "wcol", None, "dom"),
        P("dom"),
        P(None, None, "dom"),
        P(),
        P("wrow", "wcol", None),
        P("dom"),
        P("dom"),
        P("dom", None),
        P("dom", None),
        P("wrow", "wcol"),
        P("wrow", "wcol"),
    )
    return jax.shard_map(
        per_device,
        mesh=mesh,
        in_specs=placed,
        out_specs=(
            P("wrow", "wcol", None, "dom"),
            P("wrow", "wcol", None, "dom"),
            P("wrow", "wcol", None, "dom"),
        ),
        check_vma=False,
    )
```

profile of v0, /device:TPU:0, one launch (start us, length us, event | category | flops | bytes accessed | tf_op | source)
XLA Modules:
  0.0 262.9 jit_solution(8583828960577028149)
XLA Ops:
  3.1 5.5 %gather_fusion = f32[2048,3]{1,0:T(8,128)S(1)} fusion(f32[3,2048]{0,1:T(8,128)S(1)} %bitcast.293, s32[2048]{0:T(1024)S(1)} %get-tuple-element.166), kind=kCustom, calls=%fused_computation | custom fusion | bytes 57344 | tf_op jit(solution)/shard_map/gather | solution.py:66
  10.2 5.6 %collective-permute-start = (f32[3,2048]{1,0:T(4,128)S(1)}, f32[3,2048]{1,0:T(4,128)S(1)}, u32[]{:S(2)}, u32[]{:S(2)}) collective-permute-start(f32[3,2048]{1,0:T(4,128)S(1)} %bitcast.295), channel_id=1, source_target_pairs={{0,1},{1,2},{2,3},{4,5},{5,6},{6,7},{8,9},{9,10},{10,11},{12,13},{... | collective-permute-start | bytes 73736 | tf_op jit(solution)/shard_map/ppermute | solution.py:24
  16.2 11.8 %gather_fusion.2 = f32[2048]{0:T(1024)S(1)} fusion(f32[2048]{0:T(1024)S(1)} %copy-done, s32[2048]{0:T(1024)S(1)} %get-tuple-element.166), kind=kCustom, calls=%fused_computation.2 | custom fusion | bytes 24576 | tf_op jit(solution)/shard_map/gather | solution.py:68
  28.1 2.3 copy.218
  30.4 8.4 %gather_fusion.5 = f32[2048,2,3]{2,1,0:T(2,128)S(1)} fusion(f32[2,3,2048]{1,0,2:T(2,128)} %copy.218, s32[2048]{0:T(1024)S(1)} %get-tuple-element.166), kind=kCustom, calls=%fused_computation.5 | custom fusion | bytes 106496 | tf_op jit(solution)/shard_map/gather | solution.py:69
  38.8 2.3 fusion.37
  41.8 10.9 %psum.28 = f32[2]{0:T(128)S(1)} all-reduce(f32[2]{0:T(128)S(1)} %fusion.37), channel_id=1, replica_groups=mesh['wrow'=4,'wcol'=2,'dom'=4] {'dom'}, use_global_device_ids=true, to_apply=%region_5.6 | all-reduce | flops 2 | bytes 16 | tf_op jit(solution)/shard_map/psum | solution.py:95
  52.7 9.9 %fusion.38 = f32[3,2048]{0,1:T(8,128)S(1)} fusion(f32[2048,2,3]{2,1,0:T(2,128)S(1)} %gather_fusion.5, f32[2]{0:T(128)S(1)} %fusion.71), kind=kLoop, calls=%fused_computation.76 | loop fusion | flops 18432 | bytes 73736 | tf_op jit(solution)/shard_map/reduce_sum | solution.py:92
  64.0 8.8 %gather_fusion.1 = f32[2048,3]{1,0:T(8,128)} fusion(f32[3,2048]{0,1:T(8,128)} %bitcast.292, s32[2048]{0:T(1024)S(1)} %get-tuple-element.166), kind=kCustom, calls=%fused_computation.1 | custom fusion | bytes 57344 | tf_op jit(solution)/shard_map/gather | solution.py:67
  72.8 1.6 copy.216
  76.4 12.3 %while.40 = (s32[]{:T(128)}, f32[2,32,3,128]{3,2,1,0:T(4,128)S(1)}, f32[2,32,3,128]{3,2,1,0:T(4,128)S(1)}, f32[2,32,3,128]{3,2,1,0:T(4,128)S(1)}, s32[]{:T(128)}) while((s32[]{:T(128)}, f32[2,32,3,128]{3,2,1,0:T(4,128)S(1)}, f32[2,32,3,128]{3,2,1,0:T(4,128)S(1)}, f32[2,32,3,128]{3,2,1,0:T(4,128)S(1)}, s32[]{:T(128)}) %tuple.101), condition=%wide.region_3.0_spmd, body=%wide.region_0.3_spmd.sunk | while | flops 25710592 | bytes 6816841 | solution.py:87
  76.5 2.1 multiply_reduce_fusion.8
  79.2 3.4 %fusion.89 = f32[2,32,3,128]{3,2,1,0:T(4,128)S(1)} fusion(f32[2,32,3,128]{3,2,1,0:T(4,128)S(1)} %get-tuple-element.289, s32[]{:T(128)S(6)} %copy.313, f32[32,128,128]{2,1,0:T(8,128)S(1)} %multiply_reduce_fusion.8, f32[32,128]{1,0:T(8,128)S(1)} %fusion.88, f32[2,32,3,128]{3,2,1,0:T(4,128)S(1)} %get-tuple-element.295, ...), kind=kOutput, calls=%fused_computation.20.clone.1 | convolution fusion | flops 19947520 | bytes 2311168 | tf_op jit(solution)/shard_map/while/body/eval_jaxpr/gcj,gij->gci/dot_general | solution.py:43
  82.6 2.1 multiply_reduce_fusion.8
  85.3 3.4 %fusion.89 = f32[2,32,3,128]{3,2,1,0:T(4,128)S(1)} fusion(f32[2,32,3,128]{3,2,1,0:T(4,128)S(1)} %get-tuple-element.289, s32[]{:T(128)S(6)} %copy.313, f32[32,128,128]{2,1,0:T(8,128)S(1)} %multiply_reduce_fusion.8, f32[32,128]{1,0:T(8,128)S(1)} %fusion.88, f32[2,32,3,128]{3,2,1,0:T(4,128)S(1)} %get-tuple-element.295, ...), kind=kOutput, calls=%fused_computation.20.clone.1 | convolution fusion | flops 19947520 | bytes 2311168 | tf_op jit(solution)/shard_map/while/body/eval_jaxpr/gcj,gij->gci/dot_general | solution.py:43
  90.6 2.3 fusion.39
  92.9 4.5 %collective-permute-start.2 = (f32[3,2048]{1,0:T(4,128)S(1)}, f32[3,2048]{1,0:T(4,128)S(1)}, u32[]{:S(2)}, u32[]{:S(2)}) collective-permute-start(f32[3,2048]{1,0:T(4,128)S(1)} %multiply_add_fusion.1), channel_id=1, source_target_pairs={{0,1},{1,2},{2,3},{4,5},{5,6},{6,7},{8,9},{9,10},{10,11},{12,13},{... | collective-permute-start | bytes 73736 | tf_op jit(solution)/shard_map/ppermute | solution.py:24
  97.4 9.2 %psum.29 = f32[2]{0:T(128)S(1)} all-reduce(f32[2]{0:T(128)S(1)} %fusion.39), channel_id=1, replica_groups=mesh['wrow'=4,'wcol'=2,'dom'=4] {'dom'}, use_global_device_ids=true, to_apply=%region_12.13 | all-reduce | flops 2 | bytes 16 | tf_op jit(solution)/shard_map/psum | solution.py:95
  106.6 9.9 %fusion.40 = f32[3,2048]{0,1:T(8,128)S(1)} fusion(f32[2048,2,3]{2,1,0:T(2,128)S(1)} %gather_fusion.5, f32[2]{0:T(128)S(1)} %fusion.72), kind=kLoop, calls=%fused_computation.78 | loop fusion | flops 18432 | bytes 73736 | tf_op jit(solution)/shard_map/reduce_sum | solution.py:92
  118.6 12.3 %while.41 = (s32[]{:T(128)}, f32[2,32,3,128]{3,2,1,0:T(4,128)S(1)}, f32[2,32,3,128]{3,2,1,0:T(4,128)S(1)}, f32[2,32,3,128]{3,2,1,0:T(4,128)S(1)}, s32[]{:T(128)}) while((s32[]{:T(128)}, f32[2,32,3,128]{3,2,1,0:T(4,128)S(1)}, f32[2,32,3,128]{3,2,1,0:T(4,128)S(1)}, f32[2,32,3,128]{3,2,1,0:T(4,128)S(1)}, s32[]{:T(128)}) %tuple.103), condition=%wide.region_10.11_spmd, body=%wide.region_7.0_spmd.sunk | while | flops 25710592 | bytes 6816841 | solution.py:87
  118.6 2.1 multiply_reduce_fusion.9
  121.3 3.4 %fusion.91 = f32[2,32,3,128]{3,2,1,0:T(4,128)S(1)} fusion(f32[2,32,3,128]{3,2,1,0:T(4,128)S(1)} %get-tuple-element.304, s32[]{:T(128)S(6)} %copy.319, f32[32,128,128]{2,1,0:T(8,128)S(1)} %multiply_reduce_fusion.9, f32[32,128]{1,0:T(8,128)S(1)} %fusion.90, f32[2,32,3,128]{3,2,1,0:T(4,128)S(1)} %get-tuple-element.310, ...), kind=kOutput, calls=%fused_computation.33.clone.1 | convolution fusion | flops 19947520 | bytes 2311168 | tf_op jit(solution)/shard_map/while/body/eval_jaxpr/gcj,gij->gci/dot_general | solution.py:43
  124.8 2.1 multiply_reduce_fusion.9
  127.5 3.4 %fusion.91 = f32[2,32,3,128]{3,2,1,0:T(4,128)S(1)} fusion(f32[2,32,3,128]{3,2,1,0:T(4,128)S(1)} %get-tuple-element.304, s32[]{:T(128)S(6)} %copy.319, f32[32,128,128]{2,1,0:T(8,128)S(1)} %multiply_reduce_fusion.9, f32[32,128]{1,0:T(8,128)S(1)} %fusion.90, f32[2,32,3,128]{3,2,1,0:T(4,128)S(1)} %get-tuple-element.310, ...), kind=kOutput, calls=%fused_computation.33.clone.1 | convolution fusion | flops 19947520 | bytes 2311168 | tf_op jit(solution)/shard_map/while/body/eval_jaxpr/gcj,gij->gci/dot_general | solution.py:43
  132.8 2.3 fusion.41
  135.1 4.5 %collective-permute-start.4 = (f32[3,2048]{1,0:T(4,128)S(1)}, f32[3,2048]{1,0:T(4,128)S(1)}, u32[]{:S(2)}, u32[]{:S(2)}) collective-permute-start(f32[3,2048]{1,0:T(4,128)S(1)} %get-tuple-element.152), channel_id=1, source_target_pairs={{0,1},{1,2},{2,3},{4,5},{5,6},{6,7},{8,9},{9,10},{10,11},{12,13},{... | collective-permute-start | bytes 73736 | tf_op jit(solution)/shard_map/ppermute | solution.py:24
  139.6 9.9 %psum.30 = f32[2]{0:T(128)S(1)} all-reduce(f32[2]{0:T(128)S(1)} %fusion.41), channel_id=1, replica_groups=mesh['wrow'=4,'wcol'=2,'dom'=4] {'dom'}, use_global_device_ids=true, to_apply=%region_19.20 | all-reduce | flops 2 | bytes 16 | tf_op jit(solution)/shard_map/psum | solution.py:95
  149.5 9.9 %fusion.42 = f32[3,2048]{0,1:T(8,128)S(1)} fusion(f32[2048,2,3]{2,1,0:T(2,128)S(1)} %gather_fusion.5, f32[2]{0:T(128)S(1)} %fusion.73), kind=kLoop, calls=%fused_computation.80 | loop fusion | flops 18432 | bytes 73736 | tf_op jit(solution)/shard_map/reduce_sum | solution.py:92
  161.5 12.3 %while.42 = (s32[]{:T(128)}, f32[2,32,3,128]{3,2,1,0:T(4,128)S(1)}, f32[2,32,3,128]{3,2,1,0:T(4,128)S(1)}, f32[2,32,3,128]{3,2,1,0:T(4,128)S(1)}, s32[]{:T(128)}) while((s32[]{:T(128)}, f32[2,32,3,128]{3,2,1,0:T(4,128)S(1)}, f32[2,32,3,128]{3,2,1,0:T(4,128)S(1)}, f32[2,32,3,128]{3,2,1,0:T(4,128)S(1)}, s32[]{:T(128)}) %tuple.105), condition=%wide.region_17.18_spmd, body=%wide.region_14.0_spmd.sunk | while | flops 25710592 | bytes 6816841 | solution.py:87
  161.6 2.1 multiply_reduce_fusion.10
  164.3 3.4 %fusion.93 = f32[2,32,3,128]{3,2,1,0:T(4,128)S(1)} fusion(f32[2,32,3,128]{3,2,1,0:T(4,128)S(1)} %get-tuple-element.319, s32[]{:T(128)S(6)} %copy.325, f32[32,128,128]{2,1,0:T(8,128)S(1)} %multiply_reduce_fusion.10, f32[32,128]{1,0:T(8,128)S(1)} %fusion.92, f32[2,32,3,128]{3,2,1,0:T(4,128)S(1)} %get-tuple-element.325, ...), kind=kOutput, calls=%fused_computation.46.clone.1 | convolution fusion | flops 19947520 | bytes 2311168 | tf_op jit(solution)/shard_map/while/body/eval_jaxpr/gcj,gij->gci/dot_general | solution.py:43
  167.7 2.1 multiply_reduce_fusion.10
  170.4 3.4 %fusion.93 = f32[2,32,3,128]{3,2,1,0:T(4,128)S(1)} fusion(f32[2,32,3,128]{3,2,1,0:T(4,128)S(1)} %get-tuple-element.319, s32[]{:T(128)S(6)} %copy.325, f32[32,128,128]{2,1,0:T(8,128)S(1)} %multiply_reduce_fusion.10, f32[32,128]{1,0:T(8,128)S(1)} %fusion.92, f32[2,32,3,128]{3,2,1,0:T(4,128)S(1)} %get-tuple-element.325, ...), kind=kOutput, calls=%fused_computation.46.clone.1 | convolution fusion | flops 19947520 | bytes 2311168 | tf_op jit(solution)/shard_map/while/body/eval_jaxpr/gcj,gij->gci/dot_general | solution.py:43
  175.7 2.3 fusion.43
  178.0 4.5 %collective-permute-start.6 = (f32[3,2048]{1,0:T(4,128)S(1)}, f32[3,2048]{1,0:T(4,128)S(1)}, u32[]{:S(2)}, u32[]{:S(2)}) collective-permute-start(f32[3,2048]{1,0:T(4,128)S(1)} %fusion.57), channel_id=1, source_target_pairs={{0,1},{1,2},{2,3},{4,5},{5,6},{6,7},{8,9},{9,10},{10,11},{12,13},{... | collective-permute-start | bytes 73736 | tf_op jit(solution)/shard_map/ppermute | solution.py:24
  182.6 9.2 %psum.31 = f32[2]{0:T(128)S(1)} all-reduce(f32[2]{0:T(128)S(1)} %fusion.43), channel_id=1, replica_groups=mesh['wrow'=4,'wcol'=2,'dom'=4] {'dom'}, use_global_device_ids=true, to_apply=%region_26.27 | all-reduce | flops 2 | bytes 16 | tf_op jit(solution)/shard_map/psum | solution.py:95
  192.0 9.9 %fusion.36 = f32[3,2048]{0,1:T(8,128)S(1)} fusion(f32[2048,2,3]{2,1,0:T(2,128)S(1)} %gather_fusion.5, f32[2]{0:T(128)S(1)} %fusion.74), kind=kLoop, calls=%fused_computation.74 | loop fusion | flops 18432 | bytes 73736 | tf_op jit(solution)/shard_map/reduce_sum | solution.py:92
  203.6 12.3 %while.43 = (s32[]{:T(128)}, f32[2,32,3,128]{3,2,1,0:T(4,128)S(1)}, f32[2,32,3,128]{3,2,1,0:T(4,128)S(1)}, f32[2,32,3,128]{3,2,1,0:T(4,128)S(1)}, s32[]{:T(128)}) while((s32[]{:T(128)}, f32[2,32,3,128]{3,2,1,0:T(4,128)S(1)}, f32[2,32,3,128]{3,2,1,0:T(4,128)S(1)}, f32[2,32,3,128]{3,2,1,0:T(4,128)S(1)}, s32[]{:T(128)}) %tuple.99), condition=%wide.region_24.25_spmd, body=%wide.region_21.0_spmd.sunk | while | flops 25710592 | bytes 6816841 | solution.py:87
  203.7 2.1 multiply_reduce_fusion.11
  206.4 3.4 %fusion.95 = f32[2,32,3,128]{3,2,1,0:T(4,128)S(1)} fusion(f32[2,32,3,128]{3,2,1,0:T(4,128)S(1)} %get-tuple-element.334, s32[]{:T(128)S(6)} %copy.331, f32[32,128,128]{2,1,0:T(8,128)S(1)} %multiply_reduce_fusion.11, f32[32,128]{1,0:T(8,128)S(1)} %fusion.94, f32[2,32,3,128]{3,2,1,0:T(4,128)S(1)} %get-tuple-element.340, ...), kind=kOutput, calls=%fused_computation.59.clone.1 | convolution fusion | flops 19947520 | bytes 2311168 | tf_op jit(solution)/shard_map/while/body/eval_jaxpr/gcj,gij->gci/dot_general | solution.py:43
  209.8 2.1 multiply_reduce_fusion.11
  212.5 3.4 %fusion.95 = f32[2,32,3,128]{3,2,1,0:T(4,128)S(1)} fusion(f32[2,32,3,128]{3,2,1,0:T(4,128)S(1)} %get-tuple-element.334, s32[]{:T(128)S(6)} %copy.331, f32[32,128,128]{2,1,0:T(8,128)S(1)} %multiply_reduce_fusion.11, f32[32,128]{1,0:T(8,128)S(1)} %fusion.94, f32[2,32,3,128]{3,2,1,0:T(4,128)S(1)} %get-tuple-element.340, ...), kind=kOutput, calls=%fused_computation.59.clone.1 | convolution fusion | flops 19947520 | bytes 2311168 | tf_op jit(solution)/shard_map/while/body/eval_jaxpr/gcj,gij->gci/dot_general | solution.py:43
  217.0 8.5 %scatter_custom_fusion = s32[2048]{0:T(1024)S(1)} fusion(s32[2048]{0:T(1024)} %get-tuple-element.165, s32[2048]{0:T(1024)S(1)} %iota.13, s32[]{:T(128)} %constant.73.clone.1), kind=kCustom, calls=%fused_computation.135 | custom fusion | bytes 8704 | tf_op jit(solution)/shard_map/scatter | solution.py:106
  225.7 1.6 collective-permute-start.9
  227.9 3.1 %collective-permute-done.9 = f32[3,3,2048]{2,1,0:T(4,128)S(1)} collective-permute-done((f32[3,3,2048]{2,1,0:T(4,128)S(1)}, f32[3,3,2048]{2,1,0:T(4,128)S(1)}, u32[]{:S(2)}, u32[]{:S(2)}) %collective-permute-start.9) | collective-permute-done | bytes 73760 | tf_op jit(solution)/shard_map/ppermute | solution.py:36
  231.1 3.1 %copy.242 = f32[3,3,2048]{1,0,2:T(4,128)} copy(f32[3,3,2048]{2,0,1:T(4,128)S(1)} %copy_select_fusion) | data formatting | bytes 147456 | tf_op jit(solution)/shard_map/jit(_where)/select_n | solution.py:112
  234.3 17.5 %gather_fusion.12 = f32[2048,3,3]{2,1,0:T(4,128)} fusion(f32[3,3,2048]{1,0,2:T(4,128)} %copy.242, s32[2048]{0:T(1024)S(1)} %fusion.64), kind=kCustom, calls=%fused_computation.12 | custom fusion | bytes 155648 | tf_op jit(solution)/shard_map/gather | solution.py:113
  251.8 7.8 %fusion.79 = (f32[1,3,2048]{1,0,2:T(1,128)S(1)}, f32[1,3,2048]{1,0,2:T(1,128)S(1)}, f32[1,3,2048]{1,0,2:T(1,128)S(1)}) fusion(f32[3,3,2048]{1,0,2:T(4,128)} %bitcast.291), kind=kLoop, calls=%fused_computation.150 | loop fusion | bytes 147456 | tf_op jit(solution)/shard_map/slice | solution.py:114
  (114 shorter events, 28.2 us)
Async XLA Ops:
  0.6 15.6 %copy-start = (f32[2048]{0:T(1024)S(1)}, f32[2048]{0:T(1024)}, u32[]{:S(2)}) copy-start(f32[2048]{0:T(1024)} %param.22) | copy-start | bytes 24580
  0.6 15.5 %copy-start.11 = (s32[1,64]{1,0:T(1,128)S(1)}, s32[1,64]{1,0:T(1,128)}, u32[]{:S(2)}) copy-start(s32[1,64]{1,0:T(1,128)} %param.29) | copy-start | bytes 772
  0.7 15.5 %copy-start.3 = (s32[1,64]{1,0:T(1,128)S(1)}, s32[1,64]{1,0:T(1,128)}, u32[]{:S(2)}) copy-start(s32[1,64]{1,0:T(1,128)} %param.28) | copy-start | bytes 772
  8.9 66.1 %collective-permute-start.1 = (f32[3,2048]{1,0:T(4,128)S(1)}, f32[3,2048]{1,0:T(4,128)S(1)}, u32[]{:S(2)}, u32[]{:S(2)}) collective-permute-start(f32[3,2048]{1,0:T(4,128)S(1)} %bitcast.294), channel_id=1, source_target_pairs={{1,0},{2,1},{3,2},{5,4},{6,5},{7,6},{9,8},{10,9},{11,10},{13,12},{... | collective-permute-start | bytes 73736 | tf_op jit(solution)/shard_map/ppermute | solution.py:26
  10.2 64.8 %collective-permute-start = (f32[3,2048]{1,0:T(4,128)S(1)}, f32[3,2048]{1,0:T(4,128)S(1)}, u32[]{:S(2)}, u32[]{:S(2)}) collective-permute-start(f32[3,2048]{1,0:T(4,128)S(1)} %bitcast.295), channel_id=1, source_target_pairs={{0,1},{1,2},{2,3},{4,5},{5,6},{6,7},{8,9},{9,10},{10,11},{12,13},{... | collective-permute-start | bytes 73736 | tf_op jit(solution)/shard_map/ppermute | solution.py:24
  16.2 11.8 %copy-start.1 = (f32[2,3,2048]{2,0,1:T(2,128)S(1)}, f32[2,3,2048]{2,0,1:T(2,128)}, u32[]{:S(2)}) copy-start(f32[2,3,2048]{2,0,1:T(2,128)} %param.23) | copy-start | bytes 147460
  30.4 22.3 %copy-start.7 = (f32[2]{0:T(128)S(1)}, f32[2]{0:T(128)}, u32[]{:S(2)}) copy-start(f32[2]{0:T(128)} %param.24) | copy-start | bytes 28
  30.4 22.3 %copy-start.9 = (f32[1,1,2]{2,1,0:T(1,128)S(1)}, f32[1,1,2]{2,1,0:T(1,128)}, u32[]{:S(2)}) copy-start(f32[1,1,2]{2,1,0:T(1,128)} %param.25) | copy-start | bytes 28
  41.1 21.5 %copy-start.2 = (f32[1,1,3,2048]{3,1,2,0:T(1,128)S(1)}, f32[1,1,3,2048]{3,1,2,0:T(1,128)}, u32[]{:S(2)}) copy-start(f32[1,1,3,2048]{3,1,2,0:T(1,128)} %param.21) | copy-start | bytes 73732
  62.6 68.2 %copy-start.5 = (pred[64]{0:T(512)(128)(4,1)}, pred[64]{0:T(512)(128)(4,1)S(1)}, u32[]{:S(2)}) copy-start(pred[64]{0:T(512)(128)(4,1)S(1)} %iota_compare_fusion.1) | copy-start | bytes 196
  88.9 28.3 %collective-permute-start.3 = (f32[3,2048]{1,0:T(4,128)S(1)}, f32[3,2048]{1,0:T(4,128)S(1)}, u32[]{:S(2)}, u32[]{:S(2)}) collective-permute-start(f32[3,2048]{1,0:T(4,128)S(1)} %multiply_add_fusion.1), channel_id=1, source_target_pairs={{1,0},{2,1},{3,2},{5,4},{6,5},{7,6},{9,8},{10,9},{11,10},{13,12},{... | collective-permute-start | bytes 73736 | tf_op jit(solution)/shard_map/ppermute | solution.py:26
  92.9 24.3 %collective-permute-start.2 = (f32[3,2048]{1,0:T(4,128)S(1)}, f32[3,2048]{1,0:T(4,128)S(1)}, u32[]{:S(2)}, u32[]{:S(2)}) collective-permute-start(f32[3,2048]{1,0:T(4,128)S(1)} %multiply_add_fusion.1), channel_id=1, source_target_pairs={{0,1},{1,2},{2,3},{4,5},{5,6},{6,7},{8,9},{9,10},{10,11},{12,13},{... | collective-permute-start | bytes 73736 | tf_op jit(solution)/shard_map/ppermute | solution.py:24
  131.1 29.0 %collective-permute-start.5 = (f32[3,2048]{1,0:T(4,128)S(1)}, f32[3,2048]{1,0:T(4,128)S(1)}, u32[]{:S(2)}, u32[]{:S(2)}) collective-permute-start(f32[3,2048]{1,0:T(4,128)S(1)} %get-tuple-element.152), channel_id=1, source_target_pairs={{1,0},{2,1},{3,2},{5,4},{6,5},{7,6},{9,8},{10,9},{11,10},{13,12},{... | collective-permute-start | bytes 73736 | tf_op jit(solution)/shard_map/ppermute | solution.py:26
  135.1 25.1 %collective-permute-start.4 = (f32[3,2048]{1,0:T(4,128)S(1)}, f32[3,2048]{1,0:T(4,128)S(1)}, u32[]{:S(2)}, u32[]{:S(2)}) collective-permute-start(f32[3,2048]{1,0:T(4,128)S(1)} %get-tuple-element.152), channel_id=1, source_target_pairs={{0,1},{1,2},{2,3},{4,5},{5,6},{6,7},{8,9},{9,10},{10,11},{12,13},{... | collective-permute-start | bytes 73736 | tf_op jit(solution)/shard_map/ppermute | solution.py:24
  161.5 12.3 %copy-start.4 = (s32[1,64]{1,0:T(1,128)S(1)}, s32[1,64]{1,0:T(1,128)}, u32[]{:S(2)}) copy-start(s32[1,64]{1,0:T(1,128)} %param.28) | copy-start | bytes 772
  161.5 12.3 %copy-start.6 = (pred[64]{0:T(512)(128)(4,1)S(1)}, pred[64]{0:T(512)(128)(4,1)}, u32[]{:S(2)}) copy-start(pred[64]{0:T(512)(128)(4,1)} %copy-done.5) | copy-start | bytes 196
  174.0 17.8 %copy-start.8 = (f32[2]{0:T(128)S(1)}, f32[2]{0:T(128)}, u32[]{:S(2)}) copy-start(f32[2]{0:T(128)} %param.24) | copy-start | bytes 28
  174.0 17.8 %copy-start.10 = (f32[1,1,2]{2,1,0:T(1,128)S(1)}, f32[1,1,2]{2,1,0:T(1,128)}, u32[]{:S(2)}) copy-start(f32[1,1,2]{2,1,0:T(1,128)} %param.25) | copy-start | bytes 28
  174.1 28.1 %collective-permute-start.7 = (f32[3,2048]{1,0:T(4,128)S(1)}, f32[3,2048]{1,0:T(4,128)S(1)}, u32[]{:S(2)}, u32[]{:S(2)}) collective-permute-start(f32[3,2048]{1,0:T(4,128)S(1)} %fusion.57), channel_id=1, source_target_pairs={{1,0},{2,1},{3,2},{5,4},{6,5},{7,6},{9,8},{10,9},{11,10},{13,12},{... | collective-permute-start | bytes 73736 | tf_op jit(solution)/shard_map/ppermute | solution.py:26
  178.0 24.2 %collective-permute-start.6 = (f32[3,2048]{1,0:T(4,128)S(1)}, f32[3,2048]{1,0:T(4,128)S(1)}, u32[]{:S(2)}, u32[]{:S(2)}) collective-permute-start(f32[3,2048]{1,0:T(4,128)S(1)} %fusion.57), channel_id=1, source_target_pairs={{0,1},{1,2},{2,3},{4,5},{5,6},{6,7},{8,9},{9,10},{10,11},{12,13},{... | collective-permute-start | bytes 73736 | tf_op jit(solution)/shard_map/ppermute | solution.py:24
  216.3 9.2 %collective-permute-start.8 = (f32[3,3,2048]{2,1,0:T(4,128)S(1)}, f32[3,3,2048]{2,1,0:T(4,128)S(1)}, u32[]{:S(2)}, u32[]{:S(2)}) collective-permute-start(f32[3,3,2048]{2,1,0:T(4,128)S(1)} %copy.238), channel_id=1, source_target_pairs={{0,8},{8,0},{16,24},{24,16},{1,9},{9,1},{17,25},{25,17},{2,10},{10... | collective-permute-start | bytes 221192 | tf_op jit(solution)/shard_map/ppermute | solution.py:36
  225.7 5.3 %collective-permute-start.9 = (f32[3,3,2048]{2,1,0:T(4,128)S(1)}, f32[3,3,2048]{2,1,0:T(4,128)S(1)}, u32[]{:S(2)}, u32[]{:S(2)}) collective-permute-start(f32[3,3,2048]{2,1,0:T(4,128)S(1)} %copy.240), channel_id=1, source_target_pairs={{0,4},{4,0},{1,5},{5,1},{2,6},{6,2},{3,7},{7,3},{8,12},{12,8},{9,1... | collective-permute-start | bytes 221192 | tf_op jit(solution)/shard_map/ppermute | solution.py:36
where the time goes:
time: 266 us; the launch traced here: 263 us
  local copies, waits for them, and re-layouts  90.5 us (34%)
  other arithmetic  72.5 us (27%)
  blocking collectives  39.2 us (15%)
  matrix products  27.8 us (10%)
  starting transfers between devices  26 us (10%)
  between operations  3.66 us (1%)
  waiting for transfers between devices  3.07 us (1%)
    reduce_sum x4, other arithmetic, force_from(): return pair - jnp.sum(pull[:, None, None] * weights, axis=0)  39.5 us
    psum x4, blocking collectives, total_force(): collective = lax.psum(local_cv(current), 'dom')  39.2 us
    dot_general x8, matrix products, pair_batch(): jnp.einsum('gcj,gij->gci', other_tiles, weight_tiles, precision=lax.Preci...  27.1 us
    ppermute x4, starting transfers between devices, extended(): lax.ppermute(tail, axis, [(i, (i + 1) % count) for i in range(ends)])  19.2 us
    gather x1, local copies, waits for them, and re-layouts, per_device(): stacked = stacked[:, :, inverse]  17.5 us
    reduce_sum x8, other arithmetic, pair_batch(): squared = jnp.sum(offsets * offsets, axis=1)  16.6 us
    gather x1, local copies, waits for them, and re-layouts, per_device(): inverse_mass = inv_mass[block_order]  11.8 us
    gather x2, local copies, waits for them, and re-layouts, per_device(): speeds = velocities[0, 0][:, block_order]  10.3 us
  transfers between devices with their start and end apart: 10, of which 1 were waited for; matrix products, arithmetic and copies ran while one was open for 36% of the time, Pallas kernels for 0%

commit v1 on v0

v1 whole, which is shorter than its diff:
```python
import functools
import math

import jax
import jax.numpy as jnp
from jax import lax
from jax.experimental import pallas as pl
from jax.experimental.pallas import tpu as pltpu
from jax.sharding import PartitionSpec as P

BLK = 128
STEPS = 3
PAIR_EPS = 0.015625
DT = 0.1
SCALE = math.sqrt(0.5 * math.log2(math.e))
MESH = pl.DeviceIdType.MESH
F32 = jnp.float32
BF16 = jnp.bfloat16


def split3(value):
    high = value.astype(BF16)
    rest = value - high.astype(F32)
    middle = rest.astype(BF16)
    low = (rest - middle.astype(F32)).astype(BF16)
    return high, middle, low


def stacked_split(value):
    return jnp.concatenate(split3(value), axis=0)


def unsplit(value, rows):
    return value[0:rows] + (value[rows : 2 * rows] + value[2 * rows : 3 * rows])


def kernel(
    sizes,
    pos, vel, mass, cvw, order, own_row, own_s, other_s, count_s, stiff_s, centers_s, arow_s, acol_s,
    out_x, out_v, out_f,
    onehot, high_block, raw, raw_w, got_x, got_v, got_aux, aux, parts, tiles, xs, vs, fs, ms, ws,
    sx_send, sx_recv, sv_send, sv_recv, sa_send, sa_recv, halo_send, halo_recv, part_send, part_recv, *nears,
):
    doms, nb, slots = sizes
    row = lax.axis_index("wrow")
    col = lax.axis_index("wcol")
    me = lax.axis_index("dom")
    row_to = row + 1 - 2 * lax.rem(row, 2)
    col_to = col + 1 - 2 * lax.rem(col, 2)
    partners = [(row_to, col, me), (row, col_to, me), (row_to, col_to, me)]
    others = [(row, col, lax.rem(me + off, doms)) for off in range(1, doms)]

    lines = lax.broadcasted_iota(jnp.int32, (8, BLK), 0)
    aux[...] = jnp.where(
        lines == 0,
        centers_s[0, 0],
        jnp.where(lines == 1, centers_s[0, 1], arow_s[0, 0].astype(F32)),
    )
    for held in nears:
        held[...] = jnp.zeros(held.shape, F32)
    barrier = pltpu.get_barrier_semaphore()
    for target in partners + others:
        pl.semaphore_signal(barrier, inc=1, device_id=target, device_id_type=MESH)
    pl.semaphore_wait(barrier, len(partners) + len(others))

    def exchange(source, target, sends, recvs):
        copies = []
        for at, partner in enumerate(partners):
            copy = pltpu.make_async_remote_copy(
                src_ref=source,
                dst_ref=target.at[at],
                send_sem=sends.at[at],
                recv_sem=recvs.at[at],
                device_id=partner,
                device_id_type=MESH,
            )
            copy.start()
            copies.append(copy)
        return copies

    aux_copies = exchange(aux, got_aux, sa_send, sa_recv)
    x_copies = exchange(pos, got_x, sx_send, sx_recv)
    v_copies = exchange(vel, got_v, sv_send, sv_recv)

    jl = lax.broadcasted_iota(jnp.int32, (BLK, BLK), 0)
    listed = order[...]
    low = lax.rem(listed, BLK)
    high_block[...] = lax.div(listed, BLK)
    for b in range(nb):
        onehot[:, b * BLK : (b + 1) * BLK] = jnp.where(low[b : b + 1, :] == jl, 1.0, 0.0).astype(BF16)
    jb_lines = lax.broadcasted_iota(jnp.int32, (nb, BLK), 0)

    def permuted(source, comps, store):
        split = stacked_split(source)

        def body(b, carry):
            at = pl.ds(pl.multiple_of(b * BLK, BLK), BLK)
            picked = jnp.dot(split, onehot[:, at], preferred_element_type=F32)
            picked = unsplit(picked, comps * nb)
            mask = high_block[pl.ds(b, 1), :] == jb_lines
            for k in range(comps):
                line = jnp.sum(jnp.where(mask, picked[k * nb : (k + 1) * nb], 0.0), axis=0, keepdims=True)
                store(k, b, line)
            return carry

        lax.fori_loop(0, nb, body, 0)

    def unpermuted(source_ref):
        def body(b, total):
            at = pl.ds(pl.multiple_of(b * BLK, BLK), BLK)
            mask = high_block[pl.ds(b, 1), :] == jb_lines
            spread = jnp.concatenate(
                [jnp.where(mask, source_ref[k, pl.ds(b, 1), :], 0.0) for k in range(3)], axis=0
            )
            return total + lax.dot_general(
                stacked_split(spread), onehot[:, at], (((1,), (1,)), ((), ())), preferred_element_type=F32
            )

        total = lax.fori_loop(0, nb, body, jnp.zeros((9 * nb, BLK), F32))
        return unsplit(total, 3 * nb).reshape(3, nb, BLK)

    for b in range(nb):
        at = slice(b * BLK, (b + 1) * BLK)
        for k in range(2):
            for c in range(3):
                raw_w[(3 * k + c) * nb + b : (3 * k + c) * nb + b + 1, :] = cvw[k, c : c + 1, at]
    raw_w[6 * nb : 7 * nb, :] = mass[...]

    def store_w(k, b, line):
        if k < 6:
            ws[k // 3, k % 3, pl.ds(b, 1), :] = line
        else:
            ms[pl.ds(b, 1), :] = line

    permuted(raw_w[...], 7, store_w)

    own_mask = (lax.broadcasted_iota(jnp.int32, (nb, slots), 0) == own_row[...]) & (
        lax.broadcasted_iota(jnp.int32, (nb, slots), 1) < count_s[0]
    )
    owner = jnp.where(own_mask, 1.0, 0.0).astype(BF16)
    owner3 = jnp.concatenate([owner, owner, owner], axis=1)

    for copy in aux_copies:
        copy.wait()
    take_row = jnp.full((8, BLK), arow_s[0, 0].astype(F32)) > 0.5
    take_col = jnp.full((8, BLK), acol_s[0, 0].astype(F32)) > 0.5
    take_far = jnp.broadcast_to(got_aux[1, 2:3, :], (8, BLK)) > 0.5

    def chosen(mine, by_row, by_col, by_both):
        far = jnp.where(take_far, by_both, by_col)
        close = jnp.where(take_row, by_row, mine)
        return jnp.where(take_col, far, close)

    centre = chosen(aux[...], got_aux[0], got_aux[1], got_aux[2])
    centres = [centre[0:1, :], centre[1:2, :]]

    def take_window(source, got):
        for c in range(3):
            for b in range(0, nb, 8):
                raw[c * nb + b : c * nb + b + 8, :] = chosen(
                    source[c, b : b + 8], got[0, c, b : b + 8], got[1, c, b : b + 8], got[2, c, b : b + 8]
                )

    for copy in x_copies:
        copy.wait()
    take_window(pos, got_x)

    def store_x(k, b, line):
        xs[k, pl.ds(b, 1), :] = line

    def store_v(k, b, line):
        vs[k, pl.ds(b, 1), :] = line

    permuted(raw[...], 3, store_x)

    def take_velocities():
        for copy in v_copies:
            copy.wait()
        take_window(vel, got_v)
        permuted(raw[...], 3, store_v)

    def force(e, meanwhile):
        near = nears[e]
        x = xs[...]
        near[1] = x * SCALE
        up = pltpu.make_async_remote_copy(
            src_ref=near.at[1],
            dst_ref=near.at[0],
            send_sem=halo_send.at[e, 0],
            recv_sem=halo_recv.at[e, 0],
            device_id=(row, col, lax.rem(me + 1, doms)),
            device_id_type=MESH,
        )
        down = pltpu.make_async_remote_copy(
            src_ref=near.at[1],
            dst_ref=near.at[2],
            send_sem=halo_send.at[e, 1],
            recv_sem=halo_recv.at[e, 1],
            device_id=(row, col, lax.rem(me + doms - 1, doms)),
            device_id_type=MESH,
        )

        @pl.when(me < doms - 1)
        def _():
            up.start()

        @pl.when(me > 0)
        def _():
            down.start()

        for k in range(2):
            part = jnp.sum(ws[k] * x, axis=0)
            parts[e, me, k] = jnp.sum(part.reshape(nb // 8, 8, BLK), axis=0)
        part_copies = []
        for at, target in enumerate(others):
            copy = pltpu.make_async_remote_copy(
                src_ref=parts.at[e, me],
                dst_ref=parts.at[e, me],
                send_sem=part_send.at[e, at],
                recv_sem=part_recv.at[e, at],
                device_id=target,
                device_id_type=MESH,
            )
            copy.start()
            part_copies.append(copy)

        meanwhile()

        @pl.when(me < doms - 1)
        def _():
            up.wait_send()
            down.wait_recv()

        @pl.when(me > 0)
        def _():
            down.wait_send()
            up.wait_recv()

        unroll = 2

        def slot(p):
            own = own_s[0, p]
            other = other_s[0, p]
            slab = lax.div(other, nb)
            block = lax.rem(other, nb)
            mine = [jnp.broadcast_to(near[1, k, pl.ds(own, 1), :], (8, BLK)) for k in range(3)]
            theirs = [jnp.broadcast_to(near[slab, k, pl.ds(block, 1), :], (8, BLK)) for k in range(3)]
            tile = jnp.where(lines == 0, theirs[0], jnp.where(lines == 1, theirs[1], theirs[2]))
            turned = jnp.transpose(tile)
            total = [None, None, None]
            for j in range(BLK // 8):
                at = slice(8 * j, 8 * j + 8)
                apart = [mine[k] - jnp.broadcast_to(turned[at, k : k + 1], (8, BLK)) for k in range(3)]
                squared = apart[0] * apart[0] + apart[1] * apart[1] + apart[2] * apart[2]
                weight = jnp.exp2(-squared)
                for k in range(3):
                    term = weight * apart[k]
                    total[k] = term if j == 0 else total[k] + term
            for k in range(3):
                tiles[k, pl.ds(p, 1), :] = jnp.sum(total[k], axis=0, keepdims=True)

        def body(i, carry):
            for u in range(unroll):
                slot(i * unroll + u)
            return carry

        lax.fori_loop(0, slots // unroll, body, 0)

        for copy in part_copies:
            copy.wait()
        sums = parts[e, 0]
        for d in range(1, doms):
            sums = sums + parts[e, d]
        pulls = []
        for k in range(2):
            collective = jnp.sum(sums[k], axis=(0, 1), keepdims=True)
            pulls.append(stiff_s[k] * (collective - centres[k]))
        for k in range(3):
            pair = jnp.dot(owner3, stacked_split(tiles[k]), preferred_element_type=F32)
            fs[k] = (PAIR_EPS / SCALE) * pair - pulls[0] * ws[0, k] - pulls[1] * ws[1, k]

    force(0, take_velocities)
    for step in range(STEPS):
        half = 0.5 * DT * ms[...]
        for k in range(3):
            v = vs[k] + half * fs[k]
            vs[k] = v
            xs[k] = xs[k] + DT * v
        if step < STEPS - 1:
            force(step + 1, lambda: None)
            for k in range(3):
                vs[k] = vs[k] + half * fs[k]

    def write_positions():
        out_x[...] = unpermuted(xs)
        out_v[...] = unpermuted(vs)

    force(STEPS, write_positions)
    forces = unpermuted(fs)
    out_f[...] = forces
    out_v[...] = out_v[...] + (0.5 * DT) * mass[...][None] * forces


def per_device(
    positions, velocities, inv_mass, cv_weight, stiffness, centers, block_order, pair_count, pair_own, pair_other,
    accept_row, accept_col,
):
    atoms = block_order.shape[0]
    nb = atoms // BLK
    slots = pair_own.shape[1]
    doms = lax.axis_size("dom")
    evals = STEPS + 1
    vmem = pl.BlockSpec(memory_space=pltpu.VMEM)
    smem = pl.BlockSpec(memory_space=pltpu.SMEM)
    dma = pltpu.SemaphoreType.DMA
    shape = jax.ShapeDtypeStruct((3, nb, BLK), F32)
    outs = pl.pallas_call(
        functools.partial(kernel, (doms, nb, slots)),
        out_shape=(shape, shape, shape),
        in_specs=[vmem] * 6 + [smem] * 7,
        out_specs=(vmem, vmem, vmem),
        scratch_shapes=[
            pltpu.VMEM((BLK, atoms), BF16),
            pltpu.VMEM((nb, BLK), jnp.int32),
            pltpu.VMEM((3 * nb, BLK), F32),
            pltpu.VMEM((7 * nb, BLK), F32),
            pltpu.VMEM((3, 3, nb, BLK), F32),
            pltpu.VMEM((3, 3, nb, BLK), F32),
            pltpu.VMEM((3, 8, BLK), F32),
            pltpu.VMEM((8, BLK), F32),
            pltpu.VMEM((evals, doms, 2, 8, BLK), F32),
            pltpu.VMEM((3, slots, BLK), F32),
            pltpu.VMEM((3, nb, BLK), F32),
            pltpu.VMEM((3, nb, BLK), F32),
            pltpu.VMEM((3, nb, BLK), F32),
            pltpu.VMEM((nb, BLK), F32),
            pltpu.VMEM((2, 3, nb, BLK), F32),
            dma((3,)), dma((3,)), dma((3,)), dma((3,)), dma((3,)), dma((3,)),
            dma((evals, 2)), dma((evals, 2)), dma((evals, doms)), dma((evals, doms)),
        ]
        + [pltpu.VMEM((3, 3, nb, BLK), F32)] * evals,
        compiler_params=pltpu.CompilerParams(collective_id=0, has_side_effects=True),
        name="windows",
    )(
        positions.reshape(3, nb, BLK), velocities.reshape(3, nb, BLK), inv_mass.reshape(nb, BLK), cv_weight, block_order.reshape(nb, BLK), pair_own,
        pair_own, pair_other, pair_count, stiffness, centers[0], accept_row, accept_col,
    )
    return tuple(out.reshape(1, 1, 3, atoms) for out in outs)


def solution(mesh):
    placed = (
        P("wrow", "wcol", None, "dom"),
        P("wrow", "wcol", None, "dom"),
        P("dom"),
        P(None, None, "dom"),
        P(),
        P("wrow", "wcol", None),
        P("dom"),
        P("dom"),
        P("dom", None),
        P("dom", None),
        P("wrow", "wcol"),
        P("wrow", "wcol"),
    )
    return jax.shard_map(
        per_device,
        mesh=mesh,
        in_specs=placed,
        out_specs=(
            P("wrow", "wcol", None, "dom"),
            P("wrow", "wcol", None, "dom"),
            P("wrow", "wcol", None, "dom"),
        ),
        check_vma=False,
    )
```

time: 266 us -> 87.7 us (0.33); the launches traced: 263 us -> 87.3 us
  local copies, waits for them, and re-layouts: 90.5 us -> 4.16 us
  Pallas kernels: 0 us -> 80.6 us
  other arithmetic: 72.5 us -> 0 us
  blocking collectives: 39.2 us -> 0 us
  matrix products: 27.8 us -> 0 us
  starting transfers between devices: 26 us -> 0 us
  waiting for transfers between devices: 3.07 us -> 0 us
    pallas_call x0 -> x1, Pallas kernels: none -> 80.6 us  [per_device(): pl.pallas_call(functools.partial(kernel, (doms, nb, slots)), out_shape=(s...]
    reduce_sum x24 -> x0, other arithmetic: 70.3 us -> none  [the longest x4 39.5 us: force_from(): return pair - jnp.sum(pull[:, None, None] * weights, axis=0)]
    gather x16 -> x0, local copies, waits for them, and re-layouts: 59.5 us -> none  [the longest x1 17.5 us: per_device(): stacked = stacked[:, :, inverse]]
    psum x4 -> x0, blocking collectives: 39.2 us -> none  [total_force(): collective = lax.psum(local_cv(current), 'dom')]
    dot_general x12 -> x0, matrix products: 27.8 us -> none  [the longest x8 27.1 us: pair_batch(): jnp.einsum('gcj,gij->gci', other_tiles, weight_tiles, precision=lax.Preci...]
    ppermute x10 -> x0, starting transfers between devices: 26 us -> none  [the longest x4 19.2 us: extended(): lax.ppermute(tail, axis, [(i, (i + 1) % count) for i in range(ends)])]
    scatter x1 -> x0, local copies, waits for them, and re-layouts: 8.48 us -> none  [per_device(): jnp.zeros((atom_dev,), jnp.int32).at[block_order]]
    slice x1 -> x0, local copies, waits for them, and re-layouts: 7.83 us -> none  [per_device(): stacked[2][None, None]]
  transfers between devices with their start and end apart: 10 -> 0, of which waited for: 1 -> 0; matrix products, arithmetic and copies ran while one was open for 36% -> 0% of each run, Pallas kernels for 0% -> 0%
where the time goes in v1:
time: 87.7 us; the launch traced here: 87.3 us
  Pallas kernels  80.6 us (92%)
  local copies, waits for them, and re-layouts  4.16 us (5%)
  between operations  2.59 us (3%)
    pallas_call x1, Pallas kernels, per_device(): pl.pallas_call(functools.partial(kernel, (doms, nb, slots)), out_shape=(s...  80.6 us
    unnamed x8, local copies, waits for them, and re-layouts  4.16 us

profile of v1, /device:TPU:0, one launch (start us, length us, event | category | flops | bytes accessed | tf_op | source)
XLA Modules:
  0.0 87.3 jit_solution(6261882361167381784)
XLA Ops:
  2.6 1.4 %copy.19.cvw = f32[2,3,2048]{2,1,0:T(4,128)} copy(f32[2,3,2048]{2,0,1:T(2,128)} %param.15) | data formatting | bytes 98304 | tf_op args[3]
  4.0 80.6 %windows.1 = (f32[3,16,128]{2,1,0:T(8,128)}, f32[3,16,128]{2,1,0:T(8,128)}, f32[3,16,128]{2,1,0:T(8,128)}) custom-call(f32[3,16,128]{2,1,0:T(8,128)} %bitcast.11, f32[3,16,128]{2,1,0:T(8,128)} %bitcast.12, f32[16,128]{1,0:T(8,128)} %bitcast.13, f32[2,3,2048]{2,1,0:T(4,128)} %copy.19.cvw, s32[16,128]{1,0:T(8,128)} %bitcast.14, s32[1,64]{1,0:T(1,128)} %own_s.1, ...), custom_call_target="tpu_custom_call" | custom-call | tf_op jit(solution)/shard_map/windows/pallas_call | solution.py:317
  84.6 0.0 copy-start.1
  84.6 1.4 %copy.29 = f32[1,1,3,2048]{3,1,2,0:T(1,128)} copy(f32[1,1,3,2048]{3,1,2,0:T(1,128)} %bitcast.10) | data formatting | bytes 49152
  86.0 0.0 copy-done.1
  86.0 0.0 copy-start
  86.0 0.6 copy.30
  86.6 0.1 copy-done
  86.7 0.6 copy.31
Async XLA Ops:
  84.6 1.4 %copy-start.1 = (f32[3,16,128]{2,1,0:T(8,128)S(1)}, f32[3,16,128]{2,1,0:T(8,128)}, u32[]{:S(2)}) copy-start(f32[3,16,128]{2,1,0:T(8,128)} %get-tuple-element.7) | copy-start | bytes 73732
  86.0 0.7 copy-start

commit v2 on v1

--- a/solution.py
+++ b/solution.py
@@ -1,6 +1,7 @@
 import functools
 import math
 
+import numpy as np
 import jax
 import jax.numpy as jnp
 from jax import lax
@@ -12,7 +13,11 @@
 STEPS = 3
 PAIR_EPS = 0.015625
 DT = 0.1
-SCALE = math.sqrt(0.5 * math.log2(math.e))
+SCALE = math.sqrt(math.log2(math.e))
+ROWS = 32
+UNROLL = 8
+OTHER_ROWS = {0: 0, 1: 1, 2: 2, 3: 3, 4: 4, 5: 5, 6: 9, 7: 9, 8: 9, 9: 6, 10: 7, 11: 8, 16: 0, 17: 1, 18: 2, 19: 3, 20: 4, 21: 5}
+OWN_ROWS = {0: 0, 1: 1, 2: 2, 3: 0, 4: 1, 5: 2, 6: 6, 7: 7, 8: 8, 9: 9, 10: 9, 11: 9, 16: 3, 17: 4, 18: 5, 19: 3, 20: 4, 21: 5}
 MESH = pl.DeviceIdType.MESH
 F32 = jnp.float32
 BF16 = jnp.bfloat16
@@ -34,11 +39,19 @@
     return value[0:rows] + (value[rows : 2 * rows] + value[2 * rows : 3 * rows])
 
 
+def placing(rows_of, nb):
+    table = np.zeros((nb, ROWS, 10, nb), np.float32)
+    for row, kind in rows_of.items():
+        for b in range(nb):
+            table[b, row, kind, b] = 1.0
+    return jnp.asarray(table.reshape(nb * ROWS, 10 * nb), BF16)
+
+
 def kernel(
     sizes,
-    pos, vel, mass, cvw, order, own_row, own_s, other_s, count_s, stiff_s, centers_s, arow_s, acol_s,
+    pos, vel, mass, cvw, order, own_row, place_own, place_other, own_s, other_s, count_s, stiff_s, centers_s, arow_s, acol_s,
     out_x, out_v, out_f,
-    onehot, high_block, raw, raw_w, got_x, got_v, got_aux, aux, parts, tiles, xs, vs, fs, ms, ws,
+    onehot, high_block, raw, raw_w, got_x, got_v, got_aux, aux, parts, tiles, others_of, turned_own, summing, xs, vs, fs, ms, ws,
     sx_send, sx_recv, sv_send, sv_recv, sa_send, sa_recv, halo_send, halo_recv, part_send, part_recv, *nears,
 ):
     doms, nb, slots = sizes
@@ -103,7 +116,7 @@
                 store(k, b, line)
             return carry
 
-        lax.fori_loop(0, nb, body, 0)
+        lax.fori_loop(0, nb, body, 0, unroll=True)
 
     def unpermuted(source_ref):
         def body(b, total):
@@ -116,7 +129,7 @@
                 stacked_split(spread), onehot[:, at], (((1,), (1,)), ((), ())), preferred_element_type=F32
             )
 
-        total = lax.fori_loop(0, nb, body, jnp.zeros((9 * nb, BLK), F32))
+        total = lax.fori_loop(0, nb, body, jnp.zeros((9 * nb, BLK), F32), unroll=True)
         return unsplit(total, 3 * nb).reshape(3, nb, BLK)
 
     for b in range(nb):
@@ -134,11 +147,18 @@
 
     permuted(raw_w[...], 7, store_w)
 
-    own_mask = (lax.broadcasted_iota(jnp.int32, (nb, slots), 0) == own_row[...]) & (
-        lax.broadcasted_iota(jnp.int32, (nb, slots), 1) < count_s[0]
-    )
-    owner = jnp.where(own_mask, 1.0, 0.0).astype(BF16)
-    owner3 = jnp.concatenate([owner, owner, owner], axis=1)
+    wide = 8 * slots
+    at_slot = lax.div(lax.broadcasted_iota(jnp.int32, (slots, wide), 1), 8)
+    spread_slots = jnp.where(at_slot == lax.broadcasted_iota(jnp.int32, (slots, wide), 0), 1.0, 0.0).astype(BF16)
+    live = lax.broadcasted_iota(jnp.int32, (8, slots), 1) < count_s[0]
+    owners = jnp.where(live, jnp.broadcast_to(own_row[...], (8, slots)).astype(F32), -1.0).astype(BF16)
+    owners = jnp.dot(owners, spread_slots, preferred_element_type=F32)[0:1, :]
+    block_line = lax.broadcasted_iota(jnp.int32, (nb, wide), 0).astype(F32)
+    row_line = lax.rem(lax.broadcasted_iota(jnp.int32, (nb, wide), 1), 8)
+    for r in range(7):
+        summing[r * nb : (r + 1) * nb, :] = jnp.where(
+            (owners == block_line) & (row_line == r), 1.0, 0.0
+        ).astype(BF16)
 
     for copy in aux_copies:
         copy.wait()
@@ -224,6 +244,29 @@
             copy.start()
             part_copies.append(copy)
 
+        def features(slab):
+            highs, middles, held = [], [], []
+            for k in range(3):
+                value = near[slab, k]
+                high = value.astype(BF16)
+                middle = (value - high.astype(F32)).astype(BF16)
+                highs.append(high)
+                middles.append(middle)
+                held.append(high.astype(F32) + middle.astype(F32))
+            norm = -0.5 * (held[0] * held[0] + held[1] * held[1] + held[2] * held[2])
+            ones = jnp.ones((nb, BLK), BF16)
+            return jnp.concatenate(highs + middles + list(split3(norm)) + [ones], axis=0), held
+
+        def place_others(slab, kinds):
+            placed = jnp.dot(place_other[...], kinds, preferred_element_type=F32).astype(BF16)
+            others_of[slab * nb : (slab + 1) * nb] = placed.reshape(nb, ROWS, BLK)
+
+        kinds, held = features(1)
+        place_others(1, kinds)
+        placed = jnp.dot(place_own[...], kinds, preferred_element_type=F32)
+        for b in range(nb):
+            turned_own[b] = jnp.transpose(placed[b * ROWS : (b + 1) * ROWS]).astype(BF16)
+
         meanwhile()
 
         @pl.when(me < doms - 1)
@@ -236,35 +279,29 @@
             down.wait_send()
             up.wait_recv()
 
-        unroll = 2
-
-        def slot(p):
-            own = own_s[0, p]
-            other = other_s[0, p]
-            slab = lax.div(other, nb)
-            block = lax.rem(other, nb)
-            mine = [jnp.broadcast_to(near[1, k, pl.ds(own, 1), :], (8, BLK)) for k in range(3)]
-            theirs = [jnp.broadcast_to(near[slab, k, pl.ds(block, 1), :], (8, BLK)) for k in range(3)]
-            tile = jnp.where(lines == 0, theirs[0], jnp.where(lines == 1, theirs[1], theirs[2]))
-            turned = jnp.transpose(tile)
-            total = [None, None, None]
-            for j in range(BLK // 8):
-                at = slice(8 * j, 8 * j + 8)
-                apart = [mine[k] - jnp.broadcast_to(turned[at, k : k + 1], (8, BLK)) for k in range(3)]
-                squared = apart[0] * apart[0] + apart[1] * apart[1] + apart[2] * apart[2]
-                weight = jnp.exp2(-squared)
-                for k in range(3):
-                    term = weight * apart[k]
-                    total[k] = term if j == 0 else total[k] + term
-            for k in range(3):
-                tiles[k, pl.ds(p, 1), :] = jnp.sum(total[k], axis=0, keepdims=True)
+        place_others(0, features(0)[0])
+        place_others(2, features(2)[0])
+
+        def slots_at(first):
+            for p in [first + u for u in range(UNROLL)]:
+                theirs = others_of[other_s[0, p]]
+                weight = jnp.exp2(jnp.dot(turned_own[own_s[0, p]], theirs, preferred_element_type=F32))
+                high = weight.astype(BF16)
+                low = (weight - high.astype(F32)).astype(BF16)
+                lines_of = theirs[0:16, :]
+                pulled = lax.dot_general(
+                    jnp.concatenate([lines_of, lines_of], axis=1),
+                    jnp.concatenate([high, low], axis=1),
+                    (((1,), (1,)), ((), ())),
+                    preferred_element_type=F32,
+                )
+                tiles[p] = pulled[0:8, :]
 
         def body(i, carry):
-            for u in range(unroll):
-                slot(i * unroll + u)
+            slots_at(i * UNROLL)
             return carry
 
-        lax.fori_loop(0, slots // unroll, body, 0)
+        lax.fori_loop(0, slots // UNROLL, body, 0)
 
         for copy in part_copies:
             copy.wait()
@@ -275,8 +312,13 @@
         for k in range(2):
             collective = jnp.sum(sums[k], axis=(0, 1), keepdims=True)
             pulls.append(stiff_s[k] * (collective - centres[k]))
+        total = sum(
+            jnp.dot(summing[...], term, preferred_element_type=F32)
+            for term in split3(tiles[...].reshape(8 * slots, BLK))[::-1]
+        )
         for k in range(3):
-            pair = jnp.dot(owner3, stacked_split(tiles[k]), preferred_element_type=F32)
+            pulled = total[k * nb : (k + 1) * nb] + total[(3 + k) * nb : (4 + k) * nb]
+            pair = held[k] * total[6 * nb : 7 * nb] - pulled
             fs[k] = (PAIR_EPS / SCALE) * pair - pulls[0] * ws[0, k] - pulls[1] * ws[1, k]
 
     force(0, take_velocities)
@@ -317,7 +359,7 @@
     outs = pl.pallas_call(
         functools.partial(kernel, (doms, nb, slots)),
         out_shape=(shape, shape, shape),
-        in_specs=[vmem] * 6 + [smem] * 7,
+        in_specs=[vmem] * 8 + [smem] * 7,
         out_specs=(vmem, vmem, vmem),
         scratch_shapes=[
             pltpu.VMEM((BLK, atoms), BF16),
@@ -329,7 +371,10 @@
             pltpu.VMEM((3, 8, BLK), F32),
             pltpu.VMEM((8, BLK), F32),
             pltpu.VMEM((evals, doms, 2, 8, BLK), F32),
-            pltpu.VMEM((3, slots, BLK), F32),
+            pltpu.VMEM((slots, 8, BLK), F32),
+            pltpu.VMEM((3 * nb, ROWS, BLK), BF16),
+            pltpu.VMEM((nb, BLK, ROWS), BF16),
+            pltpu.VMEM((7 * nb, 8 * slots), BF16),
             pltpu.VMEM((3, nb, BLK), F32),
             pltpu.VMEM((3, nb, BLK), F32),
             pltpu.VMEM((3, nb, BLK), F32),
@@ -343,7 +388,7 @@
         name="windows",
     )(
         positions.reshape(3, nb, BLK), velocities.reshape(3, nb, BLK), inv_mass.reshape(nb, BLK), cv_weight, block_order.reshape(nb, BLK), pair_own,
-        pair_own, pair_other, pair_count, stiffness, centers[0], accept_row, accept_col,
+        placing(OWN_ROWS, nb), placing(OTHER_ROWS, nb), pair_own, pair_other, pair_count, stiffness, centers[0], accept_row, accept_col,
     )
     return tuple(out.reshape(1, 1, 3, atoms) for out in outs)
 

time: 87.7 us -> 58.5 us (0.67)
  Pallas kernels: 80.6 us -> 51.4 us
    pallas_call x1, Pallas kernels: 80.6 us -> 51.4 us  [per_device(): pl.pallas_call(functools.partial(kernel, (doms, nb, slots)), out_shape=(s...]
where the time goes in v2:
time: 58.5 us; the launch traced here: 58.2 us
  Pallas kernels  51.4 us (88%)
  local copies, waits for them, and re-layouts  4.16 us (7%)
  between operations  2.59 us (4%)
    pallas_call x1, Pallas kernels, per_device(): pl.pallas_call(functools.partial(kernel, (doms, nb, slots)), out_shape=(s...  51.4 us
    unnamed x8, local copies, waits for them, and re-layouts  4.16 us

profile of v2, /device:TPU:0, one launch (start us, length us, event | category | flops | bytes accessed | tf_op | source)
XLA Modules:
  0.0 58.2 jit_solution(14412870263110778981)
XLA Ops:
  2.6 1.4 %copy.21.cvw = f32[2,3,2048]{2,1,0:T(4,128)} copy(f32[2,3,2048]{2,0,1:T(2,128)} %param.17) | data formatting | bytes 98304 | tf_op args[3]
  4.0 51.4 %windows.1 = (f32[3,16,128]{2,1,0:T(8,128)}, f32[3,16,128]{2,1,0:T(8,128)}, f32[3,16,128]{2,1,0:T(8,128)}) custom-call(f32[3,16,128]{2,1,0:T(8,128)} %bitcast.8, f32[3,16,128]{2,1,0:T(8,128)} %bitcast.9, f32[16,128]{1,0:T(8,128)} %bitcast.13, f32[2,3,2048]{2,1,0:T(4,128)} %copy.21.cvw, s32[16,128]{1,0:T(8,128)} %bitcast.14, s32[1,64]{1,0:T(1,128)} %own_s.1, ...), custom_call_target="tpu_custom_call" | custom-call | tf_op jit(solution)/shard_map/windows/pallas_call | solution.py:359
  55.4 0.0 copy-start.1
  55.5 1.4 %copy.31 = f32[1,1,3,2048]{3,1,2,0:T(1,128)} copy(f32[1,1,3,2048]{3,1,2,0:T(1,128)} %bitcast.12) | data formatting | bytes 49152
  56.8 0.0 copy-done.1
  56.8 0.0 copy-start
  56.8 0.6 %copy.32 = f32[1,1,3,2048]{3,1,2,0:T(1,128)} copy(f32[1,1,3,2048]{3,1,2,0:T(1,128)S(1)} %bitcast.11) | data formatting | bytes 49152
  57.4 0.1 copy-done
  57.6 0.6 %copy.33 = f32[1,1,3,2048]{3,1,2,0:T(1,128)} copy(f32[1,1,3,2048]{3,1,2,0:T(1,128)S(1)} %bitcast.10) | data formatting | bytes 49152
Async XLA Ops:
  55.4 1.4 %copy-start.1 = (f32[3,16,128]{2,1,0:T(8,128)S(1)}, f32[3,16,128]{2,1,0:T(8,128)}, u32[]{:S(2)}) copy-start(f32[3,16,128]{2,1,0:T(8,128)} %get-tuple-element.7) | copy-start | bytes 73732
  56.8 0.7 %copy-start = (f32[3,16,128]{2,1,0:T(8,128)S(1)}, f32[3,16,128]{2,1,0:T(8,128)}, u32[]{:S(2)}) copy-start(f32[3,16,128]{2,1,0:T(8,128)} %get-tuple-element.8) | copy-start | bytes 73732
